TPU v7x, 32 devices: a whole 2x2x4 slice. The times are simulated.
32 devices in a mesh: gx: 2 (over y), gy: 4 (over z), gz: 4 (over x, core).
Axes of the slice: x: 2, y: 2, z: 4, core: 2. Of those that a mesh axis runs over, the one named last changes fastest.
Arguments:
- node_latent: bfloat16 [2, 4, 4, 512, 128], P('gx', 'gy', 'gz'), may hold values from -6 to 6
- ghost_latent: bfloat16 [2, 4, 4, 6, 64, 128], P('gx', 'gy', 'gz'), may hold values from -6 to 6
- edge_latent: bfloat16 [2, 4, 4, 2816, 128], P('gx', 'gy', 'gz'), may hold values from -6 to 6
- senders: int32 [2, 4, 4, 2816], P('gx', 'gy', 'gz'), may hold values from 0 to 895
- receivers: int32 [2, 4, 4, 2816], P('gx', 'gy', 'gz'), may hold values from 0 to 511, never falling along the last dimension, each value on 1 to 12 neighbouring positions
- export_rows: int32 [2, 4, 4, 6, 64], P('gx', 'gy', 'gz'), may hold values from 0 to 512, as said below
- node_cotangent: bfloat16 [2, 4, 4, 512, 128], P('gx', 'gy', 'gz'), may hold values from -6 to 6
- edge_cotangent: bfloat16 [2, 4, 4, 2816, 128], P('gx', 'gy', 'gz'), may hold values from -6 to 6
- w_edge_in: bfloat16 [384, 128], replicated, may hold values from -0.3125 to 0.3125
- w_edge_hidden: bfloat16 [2, 128, 128], replicated, may hold values from -0.5 to 0.5
- b_edge: float32 [3, 128], replicated, may hold values from -3 to 3
- gain_edge: float32 [128], replicated, may hold values from 0.1 to 1.9
- shift_edge: float32 [128], replicated, may hold values from -3 to 3
- w_node_in: bfloat16 [256, 128], replicated, may hold values from -0.375 to 0.375
- w_node_hidden: bfloat16 [2, 128, 128], replicated, may hold values from -0.5 to 0.5
- b_node: float32 [3, 128], replicated, may hold values from -3 to 3
- gain_node: float32 [128], replicated, may hold values from 0.1 to 1.9
Outputs:
- node_grad: float32 [2, 4, 4, 512, 128], P('gx', 'gy', 'gz')
- edge_grad: bfloat16 [2, 4, 4, 2816, 128], P('gx', 'gy', 'gz')
- grad_w_edge_in: float32 [384, 128], replicated
- grad_w_edge_hidden: float32 [2, 128, 128], replicated
- grad_b_edge: float32 [3, 128], replicated
- grad_gain_edge: float32 [128], replicated
- grad_shift_edge: float32 [128], replicated
- grad_w_node_in: float32 [256, 128], replicated
- grad_w_node_hidden: float32 [2, 128, 128], replicated
- grad_b_node: float32 [3, 128], replicated
- grad_gain_node: float32 [128], replicated
Inputs may be any that keep to these rules, and one draw needn't show every extreme that they name: `export_rows`: for each block and face the leading slots hold distinct owned rows of that block; the remaining slots hold 512, marking an empty slot.
All inputs are finite; a program needn't handle non-finite values.
Results may differ from a plain program's by a relative error of at most 0.02.
Values sent between devices are 32-bit elements; how exact they have to be, the bound alone decides.
No kernel may reach another device: no remote copies, remote signals or barrier semaphores. Data moves between devices by JAX's collectives and lax.ppermute only.
A program may use at most 64 MiB of HBM per device.

v0:
```python
import jax
import jax.numpy as jnp
from jax import lax
from jax.sharding import PartitionSpec as P

EPSILON = 1e-05


def from_behind(x, axis, by):
    peers = lax.axis_size(axis)
    return lax.ppermute(x, axis, [(i, (i + by) % peers) for i in range(peers)])


def matmul(left, right):
    return jnp.dot(left, right, preferred_element_type=jnp.float32)


def contract_rows(left, right):
    return lax.dot_general(
        left, right, (((0,), (0,)), ((), ())), preferred_element_type=jnp.float32
    )


def silu_parts(preact):
    sigmoid = jax.nn.sigmoid(preact)
    return (preact * sigmoid, sigmoid * (1.0 + preact * (1.0 - sigmoid)))


def norm_parts(preact):
    centred = preact - jnp.mean(preact, -1, keepdims=True)
    inv_std = lax.rsqrt(jnp.mean(centred * centred, -1, keepdims=True) + EPSILON)
    return (centred * inv_std, inv_std)


def norm_back(grad_out, gain, normed, inv_std):
    scaled = grad_out * gain
    return inv_std * (
        scaled
        - jnp.mean(scaled, -1, keepdims=True)
        - normed * jnp.mean(scaled * normed, -1, keepdims=True)
    )


def mlp_forward(inputs, w_first, w_hidden, biases):
    first_pre = matmul(inputs, w_first) + biases[0]
    first_act, first_slope = silu_parts(first_pre)
    first_out = first_act.astype(jnp.bfloat16)
    second_pre = matmul(first_out, w_hidden[0]) + biases[1]
    second_act, second_slope = silu_parts(second_pre)
    second_out = second_act.astype(jnp.bfloat16)
    final_pre = matmul(second_out, w_hidden[1]) + biases[2]
    return ((first_out, second_out, first_slope, second_slope), final_pre)


def mlp_back_inputs(final_grad, saved, w_first, w_hidden):
    first_out, second_out, first_slope, second_slope = saved
    final_round = final_grad.astype(jnp.bfloat16)
    second_grad = matmul(final_round, w_hidden[1].T) * second_slope
    second_round = second_grad.astype(jnp.bfloat16)
    first_grad = matmul(second_round, w_hidden[0].T) * first_slope
    first_round = first_grad.astype(jnp.bfloat16)
    input_grad = matmul(first_round, w_first.T)
    bias_grad = jnp.stack([jnp.sum(first_grad, 0), jnp.sum(second_grad, 0), jnp.sum(final_grad, 0)])
    return ((first_round, second_round, final_round), bias_grad, input_grad)


def mlp_back_weights(inputs, saved, rounded):
    first_weight = contract_rows(inputs, rounded[0])
    hidden_weight = jnp.stack(
        [contract_rows(saved[0], rounded[1]), contract_rows(saved[1], rounded[2])]
    )
    return (first_weight, hidden_weight)


def forward_states(node_rows, ghost_rows, edge_rows, sender_ids, receiver_ids, params):
    node_count, feature_width = node_rows.shape
    full_rows = jnp.concatenate([node_rows, ghost_rows.reshape(-1, feature_width)], 0)
    edge_inputs = jnp.concatenate([edge_rows, full_rows[sender_ids], full_rows[receiver_ids]], 1)
    edge_stored_state, edge_pre = mlp_forward(edge_inputs, params[0], params[1], params[2])
    edge_normed, edge_inv = norm_parts(edge_pre)
    edge_new = (edge_normed * params[3] + params[4]).astype(jnp.bfloat16)
    aggregate = jax.ops.segment_sum(
        edge_new.astype(jnp.float32), receiver_ids, num_segments=node_count
    ).astype(jnp.bfloat16)
    node_input_rows = jnp.concatenate([node_rows, aggregate], 1)
    node_saved, node_pre = mlp_forward(node_input_rows, params[5], params[6], params[7])
    node_normed, node_inv = norm_parts(node_pre)
    return (
        (edge_inputs, edge_stored_state, edge_normed, edge_inv),
        (node_input_rows, node_saved, node_normed, node_inv),
    )


def node_backward(node_state, node_cot, params):
    node_input_rows, node_saved, node_normed, node_inv = node_state
    upstream = node_cot.astype(jnp.float32)
    gain_grad = jnp.sum(upstream * node_normed, 0)
    final_grad = norm_back(upstream, params[8], node_normed, node_inv)
    rounded, bias_grad, input_grad = mlp_back_inputs(final_grad, node_saved, params[5], params[6])
    first_weight, hidden_weight = mlp_back_weights(node_input_rows, node_saved, rounded)
    return (input_grad, (first_weight, hidden_weight, bias_grad, gain_grad))


def edge_backward_inputs(
    edge_state, edge_cot, agg_grad, sender_ids, receiver_ids, total_rows, params
):
    edge_inputs, edge_stored_state, edge_normed, edge_inv = edge_state
    feature_width = edge_cot.shape[1]
    edge_upstream = edge_cot.astype(jnp.float32)
    new_grad = edge_upstream + agg_grad[receiver_ids]
    gain_grad = jnp.sum(new_grad * edge_normed, 0)
    shift_grad = jnp.sum(new_grad, 0)
    final_grad = norm_back(new_grad, params[3], edge_normed, edge_inv)
    rounded, bias_grad, input_grad = mlp_back_inputs(
        final_grad, edge_stored_state, params[0], params[1]
    )
    edge_grad = (edge_upstream + input_grad[:, :feature_width]).astype(jnp.bfloat16)
    full_grad = jax.ops.segment_sum(
        input_grad[:, feature_width : 2 * feature_width], sender_ids, num_segments=total_rows
    )
    full_grad = full_grad + jax.ops.segment_sum(
        input_grad[:, 2 * feature_width :], receiver_ids, num_segments=total_rows
    )
    return (edge_grad, full_grad, rounded, (bias_grad, gain_grad, shift_grad))


def send_back(ghost_grad):
    returned = []
    for side_index in range(2):
        returned.append(from_behind(ghost_grad[side_index], "gx", 1 - 2 * side_index))
    for side_index in range(2):
        returned.append(from_behind(ghost_grad[2 + side_index], "gy", 1 - 2 * side_index))
    for side_index in range(2):
        returned.append(from_behind(ghost_grad[4 + side_index], "gz", 1 - 2 * side_index))
    return returned


def on_device(
    node_latent,
    ghost_latent,
    edge_latent,
    senders,
    receivers,
    export_rows,
    node_cotangent,
    edge_cotangent,
    w_edge_in,
    w_edge_hidden,
    b_edge,
    gain_edge,
    shift_edge,
    w_node_in,
    w_node_hidden,
    b_node,
    gain_node,
):
    params = (
        w_edge_in,
        w_edge_hidden,
        b_edge,
        gain_edge,
        shift_edge,
        w_node_in,
        w_node_hidden,
        b_node,
        gain_node,
    )
    node_count = node_latent.shape[3]
    feature_width = node_latent.shape[4]
    node_rows = node_latent.reshape(node_count, feature_width)
    ghost_rows = ghost_latent.reshape(ghost_latent.shape[3:])
    edge_rows = edge_latent.reshape(edge_latent.shape[3:])
    edge_count = edge_rows.shape[0]
    sender_ids = senders.reshape(edge_count)
    receiver_ids = receivers.reshape(edge_count)
    face_rows = export_rows.reshape(export_rows.shape[3:])
    node_cot = node_cotangent.reshape(node_count, feature_width)
    edge_cot = edge_cotangent.reshape(edge_count, feature_width)
    devices = lax.axis_size("gx") * lax.axis_size("gy") * lax.axis_size("gz")
    edge_scale = float(edge_count * devices) ** (-0.5)
    node_scale = float(node_count * devices) ** (-0.5)
    total_rows = node_count + ghost_rows.shape[0] * ghost_rows.shape[1]
    edge_state, node_state = forward_states(
        node_rows, ghost_rows, edge_rows, sender_ids, receiver_ids, params
    )
    node_input_grad, node_weights = node_backward(node_state, node_cot, params)
    edge_grad, full_grad, rounded, edge_small = edge_backward_inputs(
        edge_state,
        edge_cot,
        node_input_grad[:, feature_width:],
        sender_ids,
        receiver_ids,
        total_rows,
        params,
    )
    ghost_grad = full_grad[node_count:].reshape(ghost_rows.shape)
    first_weight, hidden_weight = mlp_back_weights(edge_state[0], edge_state[1], rounded)
    returned = send_back(ghost_grad)
    edge_weights = (first_weight, hidden_weight) + edge_small
    summed = tuple(lax.psum(edge_weights + node_weights, ("gx", "gy", "gz")))
    edge_weights = summed[:5]
    node_weights = summed[5:]
    local_grad = (
        node_cot.astype(jnp.float32) + node_input_grad[:, :feature_width] + full_grad[:node_count]
    )
    for face_index in range(6):
        local_grad = local_grad.at[face_rows[face_index]].add(returned[face_index], mode="drop")
    node_grad = local_grad.reshape(node_latent.shape)
    edge_out = edge_grad.reshape(edge_latent.shape)
    return (
        node_grad,
        edge_out,
        edge_weights[0] * edge_scale,
        edge_weights[1] * edge_scale,
        edge_weights[2] * edge_scale,
        edge_weights[3] * edge_scale,
        edge_weights[4] * edge_scale,
        node_weights[0] * node_scale,
        node_weights[1] * node_scale,
        node_weights[2] * node_scale,
        node_weights[3] * node_scale,
    )


def solution(mesh):
    in_specs = (
        P("gx", "gy", "gz", None, None),
        P("gx", "gy", "gz", None, None, None),
        P("gx", "gy", "gz", None, None),
        P("gx", "gy", "gz", None),
        P("gx", "gy", "gz", None),
        P("gx", "gy", "gz", None, None),
        P("gx", "gy", "gz", None, None),
        P("gx", "gy", "gz", None, None),
        P(),
        P(),
        P(),
        P(),
        P(),
        P(),
        P(),
        P(),
        P(),
    )
    out_specs = (
        P("gx", "gy", "gz", None, None),
        P("gx", "gy", "gz", None, None),
        P(),
        P(),
        P(),
        P(),
        P(),
        P(),
        P(),
        P(),
        P(),
    )
    return jax.shard_map(
        on_device, mesh=mesh, in_specs=in_specs, out_specs=out_specs, check_vma=False
    )
```

profile of v0, /device:TPU:0, one launch (start us, length us, event | category | flops | bytes accessed | tf_op | source)
XLA Modules:
  0.0 269.4 jit_solution(13626993164029481154)
XLA Ops:
  8.0 1.3 reduce.3
  14.5 5.6 %gather_fusion.1 = bf16[2816,128]{1,0:T(8,128)(2,1)S(1)} fusion(bf16[896,128]{1,0:T(8,128)(2,1)S(1)} %pad_maximum_fusion.4, s32[3072]{0:T(1024)S(1)} %get-tuple-element.88), kind=kCustom, calls=%fused_computation.1 | custom fusion | bytes 1453056 | tf_op jit(solution)/shard_map/gather | solution.py:78
  20.1 5.6 %gather_fusion = bf16[2816,128]{1,0:T(8,128)(2,1)S(1)} fusion(bf16[896,128]{1,0:T(8,128)(2,1)S(1)} %pad_maximum_fusion.4, s32[3072]{0:T(1024)S(1)} %pad_clamp_fusion.2), kind=kCustom, calls=%fused_computation | custom fusion | bytes 1453056 | tf_op jit(solution)/shard_map/gather | solution.py:78
  25.7 1.1 copy.40
  26.9 1.9 convolution_add_fusion.2
  32.0 1.6 copy.38
  33.6 19.6 %scatter_custom_fusion = f32[512,128]{1,0:T(8,128)S(1)} fusion(s32[2816]{0:T(1024)S(1)} %reduce, f32[2816,128]{1,0:T(8,128)} %copy.38, f32[]{:T(128)} %constant.8.clone.1), kind=kCustom, calls=%fused_computation.79 | custom fusion | flops 360448 | bytes 262656 | tf_op jit(solution)/shard_map/scatter-add | solution.py:82
  56.9 5.9 %gather_fusion.2 = f32[2816,128]{1,0:T(8,128)} fusion(f32[512,128]{1,0:T(8,128)S(1)} %get-tuple-element.54, s32[3072]{0:T(1024)S(1)} %get-tuple-element.87), kind=kCustom, calls=%fused_computation.2 | custom fusion | bytes 2894848 | tf_op jit(solution)/shard_map/gather | solution.py:110
  62.8 1.8 copy.41
  64.6 3.1 %multiply_reduce_fusion = (f32[128]{0:T(128)}, f32[2816]{0:T(1024)S(1)}, f32[2816]{0:T(1024)S(1)}, f32[128]{0:T(128)}) fusion(f32[2816,128]{0,1:T(8,128)S(1)} %get-tuple-element.76, f32[2816]{0:T(1024)S(1)} %add_rsqrt_fusion, f32[2816]{0:T(1024)S(1)} %broadcast_multiply_fusion.6, f32[2816,128]{0,1:T(8,128)S(1)} %copy.41, ...), kind=kLoop, calls=%fused_computation.25 | loop fusion | flops 3959040 | bytes 3651072 | tf_op jit(solution)/shard_map/reduce_sum | solution.py:111
  69.2 1.3 fusion.73
  70.5 1.3 fusion.74
  71.8 2.7 %fusion.12 = f32[2816,384]{1,0:T(8,128)} fusion(bf16[384,128]{1,0:T(8,128)(2,1)S(1)} %copy-done, bf16[2816,128]{1,0:T(8,128)(2,1)S(1)} %get-tuple-element.82), kind=kOutput, calls=%fused_computation.55 | convolution fusion | flops 276824064 | bytes 5144576 | tf_op jit(solution)/shard_map/dot_general | solution.py:15
  74.5 19.4 %scatter_custom_fusion.2 = f32[896,128]{1,0:T(8,128)S(1)} fusion(s32[2816]{0:T(1024)} %copy-done.23, f32[2816,384]{1,0:T(8,128)} %fusion.12, f32[]{:T(128)} %constant.8.clone.1), kind=kCustom, calls=%fused_computation.21 | custom fusion | flops 360448 | bytes 1901056 | tf_op jit(solution)/shard_map/scatter-add | solution.py:121
  94.1 15.9 %scatter_custom_fusion.1 = f32[896,128]{1,0:T(8,128)S(1)} fusion(s32[2816]{0:T(1024)} %reduce.3, f32[2816,384]{1,0:T(8,128)} %fusion.12, f32[]{:T(128)} %constant.8.clone.1), kind=kCustom, calls=%fused_computation.23 | custom fusion | flops 360448 | bytes 1901056 | tf_op jit(solution)/shard_map/scatter-add | solution.py:118
  111.1 2.4 collective-permute-start.5
  113.5 3.6 %collective-permute-start.3 = (f32[64,128]{0,1:T(8,128)}, f32[64,128]{0,1:T(8,128)}, u32[]{:S(2)}, u32[]{:S(2)}) collective-permute-start(f32[64,128]{0,1:T(8,128)} %get-tuple-element.58), channel_id=1, source_target_pairs={{0,12},{4,0},{8,4},{12,8},{1,13},{5,1},{9,5},{13,9},{2,14},{6,2},{... | collective-permute-start | bytes 98312 | tf_op jit(solution)/shard_map/ppermute | solution.py:11
  117.2 1.6 collective-permute-start
  123.4 1.4 fusion.5
  128.0 1.6 copy.54
  129.6 1.6 fusion.7
  131.5 39.2 %all-reduce = (f32[3,128]{1,0:T(4,128)S(1)}, f32[128]{0:T(128)S(1)}, f32[128]{0:T(128)S(1)}, f32[3,128]{1,0:T(4,128)S(1)}, f32[128]{0:T(128)S(1)}) all-reduce(f32[3,128]{1,0:T(4,128)S(1)} %pad_maximum_fusion.9, f32[128]{0:T(128)S(1)} %copy-done.31, f32[128]{0:T(128)S(1)} %copy-done.32, ...), channel_id=1, replica_groups=mesh['gx'=2,'gy'=4,'gz'=4] {'gx','gy','gz'}, use_global_device_ids=true, to_apply=%region_22.0 | all-reduce | flops 1152 | bytes 9216 | tf_op jit(solution)/shard_map/psum | solution.py:200
  173.0 2.3 collective-permute-start.1
  175.8 1.1 copy.52
  177.9 1.0 scatter_fusion
  179.0 1.0 scatter_fusion.1
  181.0 1.0 scatter_fusion.2
  188.0 68.3 %all-reduce.4.cloned.1.call-done = (f32[384,128]{1,0:T(8,128)}, f32[2,128,128]{2,1,0:T(8,128)}, f32[256,128]{1,0:T(8,128)}, f32[2,128,128]{2,1,0:T(8,128)}) async-done(((f32[384,128]{1,0:T(8,128)}, f32[2,128,128]{2,1,0:T(8,128)}, f32[256,128]{1,0:T(8,128)}, f32[2,128,128]{2,1,0:T(8,128)}), (f32[384,128]{1,0:T(8,128)}, f32[2,128,128]{2,1,0:T(8,128)}, f32[256,128]{1,0:T(8,128)}, ...) | async-done | bytes 589840 | tf_op jit(solution)/shard_map/psum | solution.py:200
  256.2 1.6 broadcast_multiply_fusion
  257.9 1.6 broadcast_multiply_fusion.3
  259.4 1.6 broadcast_multiply_fusion.2
  261.0 1.6 broadcast_multiply_fusion.1
  (185 shorter events, 34.0 us)
Async XLA Ops:
  7.2 19.7 %copy-start = (bf16[384,128]{1,0:T(8,128)(2,1)S(1)}, bf16[384,128]{1,0:T(8,128)(2,1)}, u32[]{:S(2)}) copy-start(bf16[384,128]{1,0:T(8,128)(2,1)} %param.25) | copy-start | bytes 294916
  7.2 249.1 %all-reduce.4.cloned.1.call-start = ((), (), s32[]{:S(2)}) async-start(), calls=%async_computation | async-start | bytes 1179648 | tf_op jit(solution)/shard_map/psum | solution.py:200
  10.1 23.5 %copy-start.23 = (s32[2816]{0:T(1024)}, s32[2816]{0:T(1024)S(1)}, u32[]{:S(2)}) copy-start(s32[2816]{0:T(1024)S(1)} %reduce) | copy-start | bytes 33796
  20.1 6.8 %copy-start.9 = (bf16[2816,128]{1,0:T(8,128)(2,1)}, bf16[2816,128]{1,0:T(8,128)(2,1)S(1)}, u32[]{:S(2)}) copy-start(bf16[2816,128]{1,0:T(8,128)(2,1)S(1)} %gather_fusion.1) | copy-start | bytes 2162692
  20.1 5.6 %copy-start.8 = (bf16[1,1,1,2816,128]{4,3,2,1,0:T(8,128)(2,1)S(1)}, bf16[1,1,1,2816,128]{4,3,2,1,0:T(8,128)(2,1)}, u32[]{:S(2)}) copy-start(bf16[1,1,1,2816,128]{4,3,2,1,0:T(8,128)(2,1)} %param.24) | copy-start | bytes 2162692
  25.7 3.0 %copy-start.11 = (bf16[2816,128]{1,0:T(8,128)(2,1)}, bf16[2816,128]{1,0:T(8,128)(2,1)S(1)}, u32[]{:S(2)}) copy-start(bf16[2816,128]{1,0:T(8,128)(2,1)S(1)} %gather_fusion) | copy-start | bytes 2162692
  32.0 21.2 %copy-start.13 = (bf16[1,1,1,512,128]{4,3,2,1,0:T(8,128)(2,1)S(1)}, bf16[1,1,1,512,128]{4,3,2,1,0:T(8,128)(2,1)}, u32[]{:S(2)}) copy-start(bf16[1,1,1,512,128]{4,3,2,1,0:T(8,128)(2,1)} %param.17) | copy-start | bytes 393220
  32.0 21.2 %copy-start.18 = (bf16[256,128]{1,0:T(8,128)(2,1)S(1)}, bf16[256,128]{1,0:T(8,128)(2,1)}, u32[]{:S(2)}) copy-start(bf16[256,128]{1,0:T(8,128)(2,1)} %param.30) | copy-start | bytes 196612
  32.0 21.4 %copy-start.39 = (bf16[2,128,128]{2,1,0:T(8,128)(2,1)S(1)}, bf16[2,128,128]{2,1,0:T(8,128)(2,1)}, u32[]{:S(2)}) copy-start(bf16[2,128,128]{2,1,0:T(8,128)(2,1)} %param.31) | copy-start | bytes 196612
  33.5 20.1 %copy-start.40 = (bf16[2,128,128]{2,1,0:T(8,128)(2,1)S(1)}, bf16[2,128,128]{2,1,0:T(8,128)(2,1)}, u32[]{:S(2)}) copy-start(bf16[2,128,128]{2,1,0:T(8,128)(2,1)} %param.31) | copy-start | bytes 196612
  64.6 3.1 %copy-start.2 = (bf16[1,1,1,2816,128]{3,4,2,1,0:T(8,128)(2,1)S(1)}, bf16[1,1,1,2816,128]{3,4,2,1,0:T(8,128)(2,1)}, u32[]{:S(2)}) copy-start(bf16[1,1,1,2816,128]{3,4,2,1,0:T(8,128)(2,1)} %copy.40) | copy-start | bytes 2162692
  68.5 1.9 copy-start.6
  110.0 8.7 %copy-start.25 = (f32[512]{0:T(512)S(1)}, f32[512]{0:T(512)}, u32[]{:S(2)}) copy-start(f32[512]{0:T(512)} %copy-done.24) | copy-start | bytes 6148
  110.0 8.7 %copy-start.30 = (f32[128]{0:T(128)S(1)}, f32[128]{0:T(128)}, u32[]{:S(2)}) copy-start(f32[128]{0:T(128)} %param.33) | copy-start | bytes 1540
  110.2 8.5 %copy-start.44 = (f32[512,128]{1,0:T(8,128)S(1)}, f32[512,128]{1,0:T(8,128)}, u32[]{:S(2)}) copy-start(f32[512,128]{1,0:T(8,128)} %copy-done.43) | copy-start | bytes 786436
  110.3 8.8 %copy-start.17 = (f32[512,128]{1,0:T(8,128)S(1)}, f32[512,128]{1,0:T(8,128)}, u32[]{:S(2)}) copy-start(f32[512,128]{1,0:T(8,128)} %copy-done.16) | copy-start | bytes 786436
  110.3 8.8 %copy-start.46 = (bf16[512,128]{1,0:T(8,128)(2,1)S(1)}, bf16[512,128]{1,0:T(8,128)(2,1)}, u32[]{:S(2)}) copy-start(bf16[512,128]{1,0:T(8,128)(2,1)} %copy-done.45) | copy-start | bytes 393220
  111.1 74.8 %collective-permute-start.5 = (f32[64,128]{0,1:T(8,128)}, f32[64,128]{0,1:T(8,128)}, u32[]{:S(2)}, u32[]{:S(2)}) collective-permute-start(f32[64,128]{0,1:T(8,128)} %get-tuple-element.56), channel_id=1, source_target_pairs={{0,3},{1,0},{2,1},{3,2},{4,7},{5,4},{6,5},{7,6},{8,11},{9,8},{10,9... | collective-permute-start | bytes 98312 | tf_op jit(solution)/shard_map/ppermute | solution.py:11
  113.5 70.5 %collective-permute-start.4 = (f32[64,128]{0,1:T(8,128)}, f32[64,128]{0,1:T(8,128)}, u32[]{:S(2)}, u32[]{:S(2)}) collective-permute-start(f32[64,128]{0,1:T(8,128)} %get-tuple-element.57), channel_id=1, source_target_pairs={{0,1},{1,2},{2,3},{3,0},{4,5},{5,6},{6,7},{7,4},{8,9},{9,10},{10,1... | collective-permute-start | bytes 98312 | tf_op jit(solution)/shard_map/ppermute | solution.py:11
  113.5 68.5 %collective-permute-start.3 = (f32[64,128]{0,1:T(8,128)}, f32[64,128]{0,1:T(8,128)}, u32[]{:S(2)}, u32[]{:S(2)}) collective-permute-start(f32[64,128]{0,1:T(8,128)} %get-tuple-element.58), channel_id=1, source_target_pairs={{0,12},{4,0},{8,4},{12,8},{1,13},{5,1},{9,5},{13,9},{2,14},{6,2},{... | collective-permute-start | bytes 98312 | tf_op jit(solution)/shard_map/ppermute | solution.py:11
  117.1 63.0 %collective-permute-start.2 = (f32[64,128]{0,1:T(8,128)}, f32[64,128]{0,1:T(8,128)}, u32[]{:S(2)}, u32[]{:S(2)}) collective-permute-start(f32[64,128]{0,1:T(8,128)} %get-tuple-element.59), channel_id=1, source_target_pairs={{0,4},{4,8},{8,12},{12,0},{1,5},{5,9},{9,13},{13,1},{2,6},{6,10},{... | collective-permute-start | bytes 98312 | tf_op jit(solution)/shard_map/ppermute | solution.py:11
  117.1 2.2 copy-start.15
  117.1 2.2 copy-start.21
  117.1 3.2 %copy-start.7 = (bf16[2816,128]{0,1:T(8,128)(2,1)S(1)}, bf16[2816,128]{0,1:T(8,128)(2,1)}, u32[]{:S(2)}) copy-start(bf16[2816,128]{0,1:T(8,128)(2,1)} %copy-done.6) | copy-start | bytes 2162692
  117.2 3.2 %copy-start.52 = (f32[2816,128]{1,0:T(8,128)S(1)}, f32[2816,128]{1,0:T(8,128)}, u32[]{:S(2)}) copy-start(f32[2816,128]{1,0:T(8,128)} %copy-done.50) | copy-start | bytes 4325380
  117.2 55.8 %collective-permute-start = (f32[64,128]{0,1:T(8,128)}, f32[64,128]{0,1:T(8,128)}, u32[]{:S(2)}, u32[]{:S(2)}) collective-permute-start(f32[64,128]{0,1:T(8,128)} %get-tuple-element.61), channel_id=1, source_target_pairs={{0,16},{16,0},{1,17},{17,1},{2,18},{18,2},{3,19},{19,3},{4,20},{20... | collective-permute-start | bytes 98312 | tf_op jit(solution)/shard_map/ppermute | solution.py:11
  129.6 1.9 copy-start.33
  129.6 1.9 copy-start.31
  129.6 1.9 copy-start.32
  129.6 43.3 %copy-start.22 = (f32[64,128]{0,1:T(8,128)S(1)}, f32[64,128]{0,1:T(8,128)}, u32[]{:S(2)}) copy-start(f32[64,128]{0,1:T(8,128)} %get-tuple-element.60) | copy-start | bytes 98308
  173.0 6.0 %collective-permute-start.1 = (f32[64,128]{0,1:T(8,128)S(1)}, f32[64,128]{0,1:T(8,128)S(1)}, u32[]{:S(2)}, u32[]{:S(2)}) collective-permute-start(f32[64,128]{0,1:T(8,128)S(1)} %copy-done.22), channel_id=1, source_target_pairs={{0,16},{16,0},{1,17},{17,1},{2,18},{18,2},{3,19},{19,3},{4,20},{20... | collective-permute-start | bytes 98312 | tf_op jit(solution)/shard_map/ppermute | solution.py:11
  187.9 74.6 %copy-start.1 = (f32[512,128]{1,0:T(8,128)}, f32[512,128]{1,0:T(8,128)S(1)}, u32[]{:S(2)}) copy-start(f32[512,128]{1,0:T(8,128)S(1)} %scatter_fusion.5) | copy-start | bytes 786436
  (31 other events, 42.1 us)
Sparse Core Ops, SparseCore 0:
  126.3 129.8 all-reduce.3
where the time goes:
time: 271 us; the launch traced here: 269 us
  other arithmetic  82.4 us (30%)
  waiting for transfers between devices  68.3 us (25%)
  local copies, waits for them, and re-layouts  39.8 us (15%)
  blocking collectives  39.2 us (14%)
  matrix products  14.9 us (5%)
  between operations  14.8 us (5%)
  starting transfers between devices  9.92 us (4%)
    psum x1, waiting for transfers between devices, on_device(): summed = tuple(lax.psum(edge_weights + node_weights, ('gx', 'gy', 'gz')))  68.3 us
    psum x1, blocking collectives, on_device(): summed = tuple(lax.psum(edge_weights + node_weights, ('gx', 'gy', 'gz')))  39.2 us
    scatter-add x1, other arithmetic, forward_states(): jax.ops.segment_sum(edge_new.astype(jnp.float32), receiver_ids, num_segme...  19.6 us
    scatter-add x1, other arithmetic, edge_backward_inputs(): jax.ops.segment_sum(input_grad[:, 2 * feature_width:], receiver_ids, num_...  19.4 us
    scatter-add x1, other arithmetic, edge_backward_inputs(): jax.ops.segment_sum(input_grad[:, feature_width:2 * feature_width], sende...  15.9 us
    unnamed x115, local copies, waits for them, and re-layouts  11 us
    dot_general x12, matrix products, matmul(): return jnp.dot(left, right, preferred_element_type=jnp.float32)  10.8 us
    ppermute x6, starting transfers between devices, from_behind(): return lax.ppermute(x, axis, [(i, (i + by) % peers) for i in range(peers)])  9.88 us
  transfers between devices with their start and end apart: 7, of which 1 were waited for; matrix products, arithmetic and copies ran while one was open for 9% of the time, Pallas kernels for 0%

commit v1 on v0

v1 whole, which is shorter than its diff:
```python
import jax
import jax.numpy as jnp
from jax import lax
from jax.experimental import pallas as pl
from jax.experimental.pallas import tpu as pltpu
from jax.sharding import PartitionSpec as P

EPSILON = 1e-05
AXES = ("gx", "gy", "gz")
BF16 = jnp.bfloat16
F32 = jnp.float32


def from_behind(x, axis, by):
    peers = lax.axis_size(axis)
    return lax.ppermute(x, axis, [(i, (i + by) % peers) for i in range(peers)])


def dot(left, right):
    return jnp.dot(left, right, preferred_element_type=F32)


def dot_t(left, right):
    return lax.dot_general(left, right, (((1,), (1,)), ((), ())), preferred_element_type=F32)


def dot_rows(left, right):
    return lax.dot_general(left, right, (((0,), (0,)), ((), ())), preferred_element_type=F32)


def hi_lo(x):
    high = x.astype(BF16)
    return high, (x - high.astype(F32)).astype(BF16)


def fold_halves(x):
    half = x.shape[1] // 2
    return x[:, :half] + x[:, half:]


def silu_parts(preact):
    sigmoid = 1.0 / (1.0 + jnp.exp(-preact))
    act = preact * sigmoid
    return act.astype(BF16), sigmoid + act * (1.0 - sigmoid)


def norm_parts(preact):
    centred = preact - jnp.mean(preact, -1, keepdims=True)
    inv_std = lax.rsqrt(jnp.mean(centred * centred, -1, keepdims=True) + EPSILON)
    return centred * inv_std, inv_std


def norm_back(grad_out, gain, normed, inv_std):
    scaled = grad_out * gain
    return inv_std * (
        scaled
        - jnp.mean(scaled, -1, keepdims=True)
        - normed * jnp.mean(scaled * normed, -1, keepdims=True)
    )


def rows8(x):
    return jnp.sum(x.reshape(x.shape[0] // 8, 8, x.shape[1]), 0)


def total(x):
    return jnp.sum(x, 0, keepdims=True)


def pick_chunk(rows):
    for size in (256, 128):
        if rows % size == 0:
            return size
    return rows


def block_kernel(edge_scale, node_scale, chunk):
    def kernel(
        node_ref,
        ghost_ref,
        edge_ref,
        snd_ref,
        rcv_ref,
        ncot_ref,
        ecot_ref,
        w1_ref,
        wh_ref,
        b_ref,
        gain_ref,
        shift_ref,
        nw1_ref,
        nwh_ref,
        nb_ref,
        ngain_ref,
        local_ref,
        ghost_out_ref,
        edge_out_ref,
        grads_ref,
        one_ref,
        one_t_ref,
        table_ref,
        z1_ref,
        z2_ref,
        s1_ref,
        s2_ref,
        n_ref,
        inv_ref,
        g1_ref,
        g2_ref,
        g3_ref,
        new_ref,
        small_ref,
    ):
        nodes, width = node_ref.shape
        ghosts = ghost_ref.shape[0]
        full_count = nodes + ghosts
        total_rows = full_count + nodes
        edges = edge_ref.shape[0]
        steps = edges // chunk
        node = node_ref[...]
        ghost = ghost_ref[...]
        w_edge = w1_ref[0:width, :]
        w_snd = w1_ref[width : 2 * width, :]
        w_rcv = w1_ref[2 * width : 3 * width, :]

        def put_table(first, value):
            high, low = hi_lo(value)
            table_ref[first : first + value.shape[0], 0:width] = high
            table_ref[first : first + value.shape[0], width : 2 * width] = low

        put_table(0, dot(node, w_snd))
        put_table(nodes, dot(ghost, w_snd))
        put_table(full_count, dot(node, w_rcv))
        small_ref[...] = jnp.zeros(small_ref.shape, F32)

        lane = lax.broadcasted_iota(jnp.int32, (chunk, width), 1)
        sub = lax.broadcasted_iota(jnp.int32, (width, chunk), 0)

        def forward(step, carry):
            start = pl.multiple_of(step * chunk, chunk)
            rows = pl.ds(start, chunk)
            snd = jnp.broadcast_to(snd_ref[:, rows], (width, chunk))
            rcv = jnp.broadcast_to(rcv_ref[:, rows], (width, chunk))
            snd_col = snd.T
            rcv_col = rcv.T
            for base in range(0, total_rows, width):
                ids, ids_col, shift = (
                    (snd, snd_col, base) if base < full_count else (rcv, rcv_col, base - full_count)
                )
                one_t_ref[base : base + width, rows] = jnp.where(
                    sub == ids - shift, 1.0, 0.0
                ).astype(BF16)
                one_ref[rows, base : base + width] = jnp.where(
                    lane == ids_col - shift, 1.0, 0.0
                ).astype(BF16)
            pre = fold_halves(dot(one_ref[rows, :], table_ref[...]))
            pre = pre + dot(edge_ref[rows, :], w_edge) + b_ref[0:1, :]
            z1, slope1 = silu_parts(pre)
            z1_ref[rows, :] = z1
            s1_ref[rows, :] = slope1
            z2, slope2 = silu_parts(dot(z1, wh_ref[0]) + b_ref[1:2, :])
            z2_ref[rows, :] = z2
            s2_ref[rows, :] = slope2
            normed, inv = norm_parts(dot(z2, wh_ref[1]) + b_ref[2:3, :])
            n_ref[rows, :] = normed
            inv_ref[rows, :] = jnp.broadcast_to(inv, (chunk, width))
            new_ref[rows, :] = (normed * gain_ref[...] + shift_ref[...]).astype(BF16)
            return carry

        lax.fori_loop(0, steps, forward, 0)

        agg = dot(one_t_ref[full_count:, :], new_ref[...]).astype(BF16)
        pre = dot(node, nw1_ref[0:width, :]) + dot(agg, nw1_ref[width:, :]) + nb_ref[0:1, :]
        nz1, ns1 = silu_parts(pre)
        nz2, ns2 = silu_parts(dot(nz1, nwh_ref[0]) + nb_ref[1:2, :])
        normed, inv = norm_parts(dot(nz2, nwh_ref[1]) + nb_ref[2:3, :])
        upstream = ncot_ref[...].astype(F32)
        node_gain = total(upstream * normed)
        grad3 = norm_back(upstream, ngain_ref[...], normed, inv)
        round3 = grad3.astype(BF16)
        grad2 = dot_t(round3, nwh_ref[1]) * ns2
        round2 = grad2.astype(BF16)
        grad1 = dot_t(round2, nwh_ref[0]) * ns1
        round1 = grad1.astype(BF16)
        local_ref[...] = upstream + dot_t(round1, nw1_ref[0:width, :])
        put_table(full_count, dot_t(round1, nw1_ref[width:, :]))

        base = 5 * width
        grads_ref[base : base + width, :] = dot_rows(node, round1) * node_scale
        grads_ref[base + width : base + 2 * width, :] = dot_rows(agg, round1) * node_scale
        grads_ref[base + 2 * width : base + 3 * width, :] = dot_rows(nz1, round2) * node_scale
        grads_ref[base + 3 * width : base + 4 * width, :] = dot_rows(nz2, round3) * node_scale

        def backward(step, carry):
            start = pl.multiple_of(step * chunk, chunk)
            rows = pl.ds(start, chunk)
            upstream = ecot_ref[rows, :].astype(F32)
            gathered = dot(one_ref[rows, full_count:], table_ref[full_count:, :])
            new_grad = upstream + fold_halves(gathered)
            normed = n_ref[rows, :]
            small_ref[3] += rows8(new_grad * normed)
            small_ref[4] += rows8(new_grad)
            grad3 = norm_back(new_grad, gain_ref[...], normed, inv_ref[rows, :])
            round3 = grad3.astype(BF16)
            g3_ref[rows, :] = round3
            small_ref[2] += rows8(grad3)
            grad2 = dot_t(round3, wh_ref[1]) * s2_ref[rows, :]
            round2 = grad2.astype(BF16)
            g2_ref[rows, :] = round2
            small_ref[1] += rows8(grad2)
            grad1 = dot_t(round2, wh_ref[0]) * s1_ref[rows, :]
            round1 = grad1.astype(BF16)
            g1_ref[rows, :] = round1
            small_ref[0] += rows8(grad1)
            edge_out_ref[rows, :] = (upstream + dot_t(round1, w_edge)).astype(BF16)
            return carry

        lax.fori_loop(0, steps, backward, 0)

        spread = dot(one_t_ref[...], g1_ref[...])
        high, low = hi_lo(spread)
        pairs = jnp.concatenate([high, low], 1)
        snd_pair = jnp.concatenate([w_snd, w_snd], 1)
        rcv_pair = jnp.concatenate([w_rcv, w_rcv], 1)
        local_ref[...] += dot_t(pairs[:nodes], snd_pair) + dot_t(pairs[full_count:], rcv_pair)
        ghost_out_ref[...] = dot_t(pairs[nodes:full_count], snd_pair)

        grads_ref[0:width, :] = dot_rows(edge_ref[...], g1_ref[...]) * edge_scale
        snd_grad = dot_rows(node, pairs[:nodes]) + dot_rows(ghost, pairs[nodes:full_count])
        grads_ref[width : 2 * width, :] = fold_halves(snd_grad) * edge_scale
        grads_ref[2 * width : 3 * width, :] = (
            fold_halves(dot_rows(node, pairs[full_count:])) * edge_scale
        )
        grads_ref[3 * width : 4 * width, :] = dot_rows(z1_ref[...], g2_ref[...]) * edge_scale
        grads_ref[4 * width : 5 * width, :] = dot_rows(z2_ref[...], g3_ref[...]) * edge_scale

        base = 9 * width
        grads_ref[base:, :] = jnp.zeros((grads_ref.shape[0] - base, width), F32)
        for index in range(5):
            grads_ref[base + index : base + index + 1, :] = total(small_ref[index]) * edge_scale
        node_small = (total(grad1), total(grad2), total(grad3), node_gain)
        for index, term in enumerate(node_small):
            grads_ref[base + 5 + index : base + 6 + index, :] = term * node_scale

    return kernel


def finish_kernel(
    local_ref,
    rows_ref,
    r0_ref,
    r1_ref,
    r2_ref,
    r3_ref,
    r4_ref,
    r5_ref,
    sums_ref,
    node_ref,
    w1_ref,
    wh_ref,
    b_ref,
    gain_ref,
    shift_ref,
    nw1_ref,
    nwh_ref,
    nb_ref,
    ngain_ref,
):
    nodes, width = local_ref.shape
    slots = rows_ref.shape[1]
    sub = lax.broadcasted_iota(jnp.int32, (nodes, slots), 0)
    added = jnp.zeros((nodes, 2 * width), F32)
    for face, ref in enumerate((r0_ref, r1_ref, r2_ref, r3_ref, r4_ref, r5_ref)):
        spots = jnp.where(sub == rows_ref[face : face + 1, :], 1.0, 0.0).astype(BF16)
        added = added + dot(spots, jnp.concatenate(hi_lo(ref[...]), 1))
    node_ref[...] = local_ref[...] + fold_halves(added)
    w1_ref[...] = sums_ref[0 : 3 * width, :]
    wh_ref[0] = sums_ref[3 * width : 4 * width, :]
    wh_ref[1] = sums_ref[4 * width : 5 * width, :]
    nw1_ref[...] = sums_ref[5 * width : 7 * width, :]
    nwh_ref[0] = sums_ref[7 * width : 8 * width, :]
    nwh_ref[1] = sums_ref[8 * width : 9 * width, :]
    base = 9 * width
    b_ref[...] = sums_ref[base : base + 3, :]
    gain_ref[...] = sums_ref[base + 3 : base + 4, :]
    shift_ref[...] = sums_ref[base + 4 : base + 5, :]
    nb_ref[...] = sums_ref[base + 5 : base + 8, :]
    ngain_ref[...] = sums_ref[base + 8 : base + 9, :]


def partner(x, axis, mask):
    return lax.ppermute(x, axis, [(i, i ^ mask) for i in range(lax.axis_size(axis))])


def masks_of(axis, reach):
    size = lax.axis_size(axis)
    if size & (size - 1):
        return None
    return [reach * 2**bit - (reach - 1) for bit in range(size.bit_length() - 1)]


def sum_blocks(x):
    halved = masks_of("gz", 1)
    if halved is None:
        return lax.psum(x, AXES)
    side = lax.axis_index("gz")
    for mask in halved:
        half = x.shape[0] // 2
        upper = (side & mask) != 0
        first, second = x[:half], x[half:]
        kept = jnp.where(upper, second, first)
        x = kept + partner(jnp.where(upper, first, second), "gz", mask)
    for axis in ("gx", "gy"):
        masks = masks_of(axis, 2)
        if masks is None:
            x = lax.psum(x, axis)
            continue
        for mask in masks:
            x = x + partner(x, axis, mask)
    for mask in reversed(halved):
        other = partner(x, "gz", mask)
        upper = (side & mask) != 0
        x = jnp.where(upper, jnp.concatenate([other, x]), jnp.concatenate([x, other]))
    return x


def on_device(
    node_latent,
    ghost_latent,
    edge_latent,
    senders,
    receivers,
    export_rows,
    node_cotangent,
    edge_cotangent,
    w_edge_in,
    w_edge_hidden,
    b_edge,
    gain_edge,
    shift_edge,
    w_node_in,
    w_node_hidden,
    b_node,
    gain_node,
):
    nodes, width = node_latent.shape[3:]
    edges = edge_latent.shape[3]
    faces, slots = export_rows.shape[3:]
    ghosts = faces * slots
    devices = 1
    for axis in AXES:
        devices *= lax.axis_size(axis)
    unit = 8 * lax.axis_size("gz")
    grad_rows = -(-(9 * width + 9) // unit) * unit
    chunk = pick_chunk(edges)
    total_rows = 2 * nodes + ghosts

    local, ghost_grad, edge_grad, grads = pl.pallas_call(
        block_kernel(
            float(edges * devices) ** (-0.5), float(nodes * devices) ** (-0.5), chunk
        ),
        out_shape=(
            jax.ShapeDtypeStruct((nodes, width), F32),
            jax.ShapeDtypeStruct((ghosts, width), F32),
            jax.ShapeDtypeStruct((edges, width), BF16),
            jax.ShapeDtypeStruct((grad_rows, width), F32),
        ),
        scratch_shapes=[
            pltpu.VMEM((edges, total_rows), BF16),
            pltpu.VMEM((total_rows, edges), BF16),
            pltpu.VMEM((total_rows, 2 * width), BF16),
            pltpu.VMEM((edges, width), BF16),
            pltpu.VMEM((edges, width), BF16),
            pltpu.VMEM((edges, width), F32),
            pltpu.VMEM((edges, width), F32),
            pltpu.VMEM((edges, width), F32),
            pltpu.VMEM((edges, width), F32),
            pltpu.VMEM((edges, width), BF16),
            pltpu.VMEM((edges, width), BF16),
            pltpu.VMEM((edges, width), BF16),
            pltpu.VMEM((edges, width), BF16),
            pltpu.VMEM((5, 8, width), F32),
        ],
        name="block_pass",
    )(
        node_latent.reshape(nodes, width),
        ghost_latent.reshape(ghosts, width),
        edge_latent.reshape(edges, width),
        senders.reshape(1, edges),
        receivers.reshape(1, edges),
        node_cotangent.reshape(nodes, width),
        edge_cotangent.reshape(edges, width),
        w_edge_in,
        w_edge_hidden,
        b_edge,
        gain_edge.reshape(1, width),
        shift_edge.reshape(1, width),
        w_node_in,
        w_node_hidden,
        b_node,
        gain_node.reshape(1, width),
    )

    returned = []
    for face in range(faces):
        slab = ghost_grad[face * slots : (face + 1) * slots]
        returned.append(from_behind(slab, AXES[face // 2], 1 - 2 * (face % 2)))
    sums = sum_blocks(grads)

    outs = pl.pallas_call(
        finish_kernel,
        out_shape=(
            jax.ShapeDtypeStruct((nodes, width), F32),
            jax.ShapeDtypeStruct((3 * width, width), F32),
            jax.ShapeDtypeStruct((2, width, width), F32),
            jax.ShapeDtypeStruct((3, width), F32),
            jax.ShapeDtypeStruct((1, width), F32),
            jax.ShapeDtypeStruct((1, width), F32),
            jax.ShapeDtypeStruct((2 * width, width), F32),
            jax.ShapeDtypeStruct((2, width, width), F32),
            jax.ShapeDtypeStruct((3, width), F32),
            jax.ShapeDtypeStruct((1, width), F32),
        ),
        name="finish",
    )(local, export_rows.reshape(faces, slots), *returned, sums)
    return (
        outs[0].reshape(node_latent.shape),
        edge_grad.reshape(edge_latent.shape),
        outs[1],
        outs[2],
        outs[3],
        outs[4].reshape(width),
        outs[5].reshape(width),
        outs[6],
        outs[7],
        outs[8],
        outs[9].reshape(width),
    )


def solution(mesh):
    block = P("gx", "gy", "gz")
    return jax.shard_map(
        on_device,
        mesh=mesh,
        in_specs=(block,) * 8 + (P(),) * 9,
        out_specs=(block, block) + (P(),) * 9,
        check_vma=False,
    )
```

time: 271 us -> 79.3 us (0.29)
  other arithmetic: 82.4 us -> 2.23 us
  waiting for transfers between devices: 68.3 us -> 22.3 us
  blocking collectives: 39.2 us -> 0 us
  local copies, waits for them, and re-layouts: 39.8 us -> 1.24 us
  Pallas kernels: 0 us -> 33 us
  matrix products: 14.9 us -> 0 us
  between operations: 14.8 us -> 0.75 us
  starting transfers between devices: 9.92 us -> 19.6 us
    psum x1 -> x0, waiting for transfers between devices: 68.3 us -> none  [on_device(): summed = tuple(lax.psum(edge_weights + node_weights, ('gx', 'gy', 'gz')))]
    scatter-add x9 -> x0, other arithmetic: 61.1 us -> none  [the longest x1 19.6 us: forward_states(): jax.ops.segment_sum(edge_new.astype(jnp.float32), receiver_ids, num_segme...]
    psum x1 -> x0, blocking collectives: 39.2 us -> none  [on_device(): summed = tuple(lax.psum(edge_weights + node_weights, ('gx', 'gy', 'gz')))]
    pallas_call x0 -> x2, Pallas kernels: none -> 33 us  [the longest x1 30.3 us: on_device(): pl.pallas_call(block_kernel(float(edges * devices) ** (-0.5), float(nodes...]
    ppermute x0 -> x7, waiting for transfers between devices: none -> 19.8 us  [partner(): lax.ppermute(x, axis, [(i, i ^ mask) for i in range(lax.axis_size(axis))])]
    gather x4 -> x0, local copies, waits for them, and re-layouts: 18.9 us -> none  [the longest x2 7.74 us: edge_backward_inputs(): new_grad = edge_upstream + agg_grad[receiver_ids]]
    dot_general x18 -> x0, matrix products: 14.9 us -> none  [the longest x12 10.8 us: matmul(): return jnp.dot(left, right, preferred_element_type=jnp.float32)]
    ppermute x0 -> x7, starting transfers between devices: none -> 12.3 us  [partner(): lax.ppermute(x, axis, [(i, i ^ mask) for i in range(lax.axis_size(axis))])]
  transfers between devices with their start and end apart: 7 -> 13, of which waited for: 1 -> 8; matrix products, arithmetic and copies ran while one was open for 9% -> 2% of each run, Pallas kernels for 0% -> 0%
where the time goes in v1:
time: 79.3 us; the launch traced here: 79.2 us
  Pallas kernels  33 us (42%)
  waiting for transfers between devices  22.3 us (28%)
  starting transfers between devices  19.6 us (25%)
  other arithmetic  2.23 us (3%)
  local copies, waits for them, and re-layouts  1.24 us (2%)
    pallas_call x1, Pallas kernels, on_device(): pl.pallas_call(block_kernel(float(edges * devices) ** (-0.5), float(nodes...  30.3 us
    ppermute x7, waiting for transfers between devices, partner(): lax.ppermute(x, axis, [(i, i ^ mask) for i in range(lax.axis_size(axis))])  19.8 us
    ppermute x7, starting transfers between devices, partner(): lax.ppermute(x, axis, [(i, i ^ mask) for i in range(lax.axis_size(axis))])  12.3 us
    ppermute x6, starting transfers between devices, from_behind(): return lax.ppermute(x, axis, [(i, (i + by) % peers) for i in range(peers)])  7.3 us
    pallas_call x1, Pallas kernels, on_device(): pl.pallas_call(finish_kernel, out_shape=(jax.ShapeDtypeStruct((nodes, wid...  2.67 us
    ppermute x6, waiting for transfers between devices, from_behind(): return lax.ppermute(x, axis, [(i, (i + by) % peers) for i in range(peers)])  2.5 us
  transfers between devices with their start and end apart: 13, of which 8 were waited for; matrix products, arithmetic and copies ran while one was open for 2% of the time, Pallas kernels for 0%

profile of v1, /device:TPU:0, one launch (start us, length us, event | category | flops | bytes accessed | tf_op | source)
XLA Modules:
  0.0 79.2 jit_solution(10129028950922259372)
XLA Ops:
  0.7 30.3 %block_pass.1 = (f32[512,128]{1,0:T(8,128)}, f32[384,128]{1,0:T(8,128)}, bf16[2816,128]{1,0:T(8,128)(2,1)}, f32[1184,128]{1,0:T(8,128)}) custom-call(bf16[512,128]{1,0:T(8,128)(2,1)} %bitcast.20, bf16[384,128]{1,0:T(8,128)(2,1)} %bitcast.22, bf16[2816,128]{1,0:T(8,128)(2,1)} %bitcast.18, s32[1,2816]{1,0:T(1,128)} %bitcast.24, s32[1,2816]{1,0:T(1,128)} %bitcast.25, ...), custom_call_target="tpu_custom_call" | custom-call | tf_op jit(solution)/shard_map/block_pass/pallas_call | solution.py:358
  31.0 1.2 %slice_select_fusion = f32[592,128]{1,0:T(8,128)S(1)} fusion(f32[1184,128]{1,0:T(8,128)} %get-tuple-element.27, pred[]{:T(512)S(6)} %ne.8), kind=kLoop, calls=%fused_computation.3 | loop fusion | flops 75776 | bytes 909313 | tf_op jit(solution)/shard_map/jit(_where)/select_n | solution.py:312
  32.1 0.6 collective-permute-start.6
  32.7 1.2 %collective-permute-done.6 = f32[592,128]{1,0:T(8,128)S(1)} collective-permute-done((f32[592,128]{1,0:T(8,128)S(1)}, f32[592,128]{1,0:T(8,128)S(1)}, u32[]{:S(2)}, u32[]{:S(2)}) %collective-permute-start.6) | collective-permute-done | bytes 303136 | tf_op jit(solution)/shard_map/ppermute | solution.py:292
  33.9 0.1 select_add_fusion
  34.0 2.9 %collective-permute-start.7 = (f32[296,128]{1,0:T(8,128)S(1)}, f32[296,128]{1,0:T(8,128)S(1)}, u32[]{:S(2)}, u32[]{:S(2)}) collective-permute-start(f32[296,128]{1,0:T(8,128)S(1)} %slice_select_fusion.1), channel_id=1, source_target_pairs={{0,2},{1,3},{2,0},{3,1},{4,6},{5,7},{6,4},{7,5},{8,10},{9,11},{10,... | collective-permute-start | bytes 454664 | tf_op jit(solution)/shard_map/ppermute | solution.py:292
  36.9 4.2 %collective-permute-done.7 = f32[296,128]{1,0:T(8,128)S(1)} collective-permute-done((f32[296,128]{1,0:T(8,128)S(1)}, f32[296,128]{1,0:T(8,128)S(1)}, u32[]{:S(2)}, u32[]{:S(2)}) %collective-permute-start.7) | collective-permute-done | bytes 151584 | tf_op jit(solution)/shard_map/ppermute | solution.py:292
  41.2 1.8 %collective-permute-start.8 = (f32[296,128]{1,0:T(8,128)S(1)}, f32[296,128]{1,0:T(8,128)S(1)}, u32[]{:S(2)}, u32[]{:S(2)}) collective-permute-start(f32[296,128]{1,0:T(8,128)S(1)} %select_add_fusion.1), channel_id=1, source_target_pairs={{0,16},{16,0},{1,17},{17,1},{2,18},{18,2},{3,19},{19,3},{4,20},{20... | collective-permute-start | bytes 454664 | tf_op jit(solution)/shard_map/ppermute | solution.py:292
  43.0 3.6 %collective-permute-done.8 = f32[296,128]{1,0:T(8,128)S(1)} collective-permute-done((f32[296,128]{1,0:T(8,128)S(1)}, f32[296,128]{1,0:T(8,128)S(1)}, u32[]{:S(2)}, u32[]{:S(2)}) %collective-permute-start.8) | collective-permute-done | bytes 151584 | tf_op jit(solution)/shard_map/ppermute | solution.py:292
  46.7 1.7 %collective-permute-start.9 = (f32[296,128]{1,0:T(8,128)S(1)}, f32[296,128]{1,0:T(8,128)S(1)}, u32[]{:S(2)}, u32[]{:S(2)}) collective-permute-start(f32[296,128]{1,0:T(8,128)S(1)} %add.17), channel_id=1, source_target_pairs={{0,4},{4,0},{8,12},{12,8},{1,5},{5,1},{9,13},{13,9},{2,6},{6,2},{1... | collective-permute-start | bytes 454664 | tf_op jit(solution)/shard_map/ppermute | solution.py:292
  48.4 3.6 %collective-permute-done.9 = f32[296,128]{1,0:T(8,128)S(1)} collective-permute-done((f32[296,128]{1,0:T(8,128)S(1)}, f32[296,128]{1,0:T(8,128)S(1)}, u32[]{:S(2)}, u32[]{:S(2)}) %collective-permute-start.9) | collective-permute-done | bytes 151584 | tf_op jit(solution)/shard_map/ppermute | solution.py:292
  52.0 3.7 %collective-permute-start.10 = (f32[296,128]{1,0:T(8,128)S(1)}, f32[296,128]{1,0:T(8,128)S(1)}, u32[]{:S(2)}, u32[]{:S(2)}) collective-permute-start(f32[296,128]{1,0:T(8,128)S(1)} %add.18), channel_id=1, source_target_pairs={{0,12},{4,8},{8,4},{12,0},{1,13},{5,9},{9,5},{13,1},{2,14},{6,10},... | collective-permute-start | bytes 454664 | tf_op jit(solution)/shard_map/ppermute | solution.py:292
  55.7 3.4 %collective-permute-done.10 = f32[296,128]{1,0:T(8,128)S(1)} collective-permute-done((f32[296,128]{1,0:T(8,128)S(1)}, f32[296,128]{1,0:T(8,128)S(1)}, u32[]{:S(2)}, u32[]{:S(2)}) %collective-permute-start.10) | collective-permute-done | bytes 151584 | tf_op jit(solution)/shard_map/ppermute | solution.py:292
  59.1 0.0 copy-start.1
  59.1 1.6 %collective-permute-start.11 = (f32[296,128]{1,0:T(8,128)S(1)}, f32[296,128]{1,0:T(8,128)S(1)}, u32[]{:S(2)}, u32[]{:S(2)}) collective-permute-start(f32[296,128]{1,0:T(8,128)S(1)} %add.19), channel_id=1, source_target_pairs={{0,2},{1,3},{2,0},{3,1},{4,6},{5,7},{6,4},{7,5},{8,10},{9,11},{10,... | collective-permute-start | bytes 454664 | tf_op jit(solution)/shard_map/ppermute | solution.py:292
  60.7 3.7 %collective-permute-done.11 = f32[296,128]{1,0:T(8,128)S(1)} collective-permute-done((f32[296,128]{1,0:T(8,128)S(1)}, f32[296,128]{1,0:T(8,128)S(1)}, u32[]{:S(2)}, u32[]{:S(2)}) %collective-permute-start.11) | collective-permute-done | bytes 151584 | tf_op jit(solution)/shard_map/ppermute | solution.py:292
  64.4 0.1 collective-permute-start.12
  64.5 0.0 copy-start.8
  64.6 1.7 %collective-permute-start.5 = (f32[64,128]{1,0:T(8,128)S(1)}, f32[64,128]{1,0:T(8,128)S(1)}, u32[]{:S(2)}, u32[]{:S(2)}) collective-permute-start(f32[64,128]{1,0:T(8,128)S(1)} %get-tuple-element.39), channel_id=1, source_target_pairs={{0,3},{1,0},{2,1},{3,2},{4,7},{5,4},{6,5},{7,6},{8,11},{9,8},{10,9... | collective-permute-start | bytes 98312 | tf_op jit(solution)/shard_map/ppermute | solution.py:16
  66.2 0.0 collective-permute-start.4
  66.2 3.6 %collective-permute-start.3 = (f32[64,128]{1,0:T(8,128)S(1)}, f32[64,128]{1,0:T(8,128)S(1)}, u32[]{:S(2)}, u32[]{:S(2)}) collective-permute-start(f32[64,128]{1,0:T(8,128)S(1)} %get-tuple-element.41), channel_id=1, source_target_pairs={{0,12},{4,0},{8,4},{12,8},{1,13},{5,1},{9,5},{13,9},{2,14},{6,2},{... | collective-permute-start | bytes 98312 | tf_op jit(solution)/shard_map/ppermute | solution.py:16
  69.8 0.0 collective-permute-start.2
  69.8 0.6 copy.30
  70.4 1.5 %collective-permute-start.1 = (f32[64,128]{1,0:T(8,128)S(1)}, f32[64,128]{1,0:T(8,128)S(1)}, u32[]{:S(2)}, u32[]{:S(2)}) collective-permute-start(f32[64,128]{1,0:T(8,128)S(1)} %get-tuple-element.43), channel_id=1, source_target_pairs={{0,16},{16,0},{1,17},{17,1},{2,18},{18,2},{3,19},{19,3},{4,20},{20... | collective-permute-start | bytes 98312 | tf_op jit(solution)/shard_map/ppermute | solution.py:16
  72.0 0.5 collective-permute-start
  72.5 0.9 %maximum_select_fusion.sums_ref = f32[1184,128]{1,0:T(8,128)} fusion(f32[592,128]{1,0:T(8,128)S(1)} %maximum_select_fusion.1, f32[592,128]{1,0:T(8,128)S(1)} %collective-permute-done.12, pred[]{:T(512)S(6)} %ne.8), kind=kLoop, calls=%fused_computation | loop fusion | flops 454656 | bytes 1212417 | tf_op jit(solution)/shard_map/jit(_where)/select_n | solution.py:323
  73.4 2.2 %collective-permute-done.2.r2_ref = f32[64,128]{1,0:T(8,128)S(1)} collective-permute-done((f32[64,128]{1,0:T(8,128)S(1)}, f32[64,128]{1,0:T(8,128)S(1)}, u32[]{:S(2)}, u32[]{:S(2)}) %collective-permute-start.2) | collective-permute-done | bytes 32800 | tf_op jit(solution)/shard_map/ppermute | solution.py:16
  75.5 0.3 collective-permute-done.r0_ref
  75.9 0.3 copy-done.5
  76.1 0.0 copy-done.6
  76.2 0.3 copy-done.7
  76.5 2.7 %finish.1 = (f32[512,128]{1,0:T(8,128)}, f32[384,128]{1,0:T(8,128)}, f32[2,128,128]{2,1,0:T(8,128)}, f32[3,128]{1,0:T(4,128)}, f32[1,128]{1,0:T(1,128)}, /*index...) custom-call(f32[512,128]{1,0:T(8,128)} %get-tuple-element.25.local_ref, ...), custom_call_target="tpu_custom_call" | custom-call | tf_op jit(solution)/shard_map/finish/pallas_call | solution.py:410
  (25 shorter events, 0.2 us)
Async XLA Ops:
  31.0 2.9 %copy-start = (f32[1184,128]{1,0:T(8,128)S(1)}, f32[1184,128]{1,0:T(8,128)}, u32[]{:S(2)}) copy-start(f32[1184,128]{1,0:T(8,128)} %get-tuple-element.27) | copy-start | bytes 1818628
  32.1 1.8 %collective-permute-start.6 = (f32[592,128]{1,0:T(8,128)S(1)}, f32[592,128]{1,0:T(8,128)S(1)}, u32[]{:S(2)}, u32[]{:S(2)}) collective-permute-start(f32[592,128]{1,0:T(8,128)S(1)} %slice_select_fusion), channel_id=1, source_target_pairs={{0,1},{1,0},{2,3},{3,2},{4,5},{5,4},{6,7},{7,6},{8,9},{9,8},{10,11... | collective-permute-start | bytes 909320 | tf_op jit(solution)/shard_map/ppermute | solution.py:292
  34.0 7.1 %collective-permute-start.7 = (f32[296,128]{1,0:T(8,128)S(1)}, f32[296,128]{1,0:T(8,128)S(1)}, u32[]{:S(2)}, u32[]{:S(2)}) collective-permute-start(f32[296,128]{1,0:T(8,128)S(1)} %slice_select_fusion.1), channel_id=1, source_target_pairs={{0,2},{1,3},{2,0},{3,1},{4,6},{5,7},{6,4},{7,5},{8,10},{9,11},{10,... | collective-permute-start | bytes 454664 | tf_op jit(solution)/shard_map/ppermute | solution.py:292
  41.2 5.5 %collective-permute-start.8 = (f32[296,128]{1,0:T(8,128)S(1)}, f32[296,128]{1,0:T(8,128)S(1)}, u32[]{:S(2)}, u32[]{:S(2)}) collective-permute-start(f32[296,128]{1,0:T(8,128)S(1)} %select_add_fusion.1), channel_id=1, source_target_pairs={{0,16},{16,0},{1,17},{17,1},{2,18},{18,2},{3,19},{19,3},{4,20},{20... | collective-permute-start | bytes 454664 | tf_op jit(solution)/shard_map/ppermute | solution.py:292
  46.7 5.3 %collective-permute-start.9 = (f32[296,128]{1,0:T(8,128)S(1)}, f32[296,128]{1,0:T(8,128)S(1)}, u32[]{:S(2)}, u32[]{:S(2)}) collective-permute-start(f32[296,128]{1,0:T(8,128)S(1)} %add.17), channel_id=1, source_target_pairs={{0,4},{4,0},{8,12},{12,8},{1,5},{5,1},{9,13},{13,9},{2,6},{6,2},{1... | collective-permute-start | bytes 454664 | tf_op jit(solution)/shard_map/ppermute | solution.py:292
  52.0 7.2 %collective-permute-start.10 = (f32[296,128]{1,0:T(8,128)S(1)}, f32[296,128]{1,0:T(8,128)S(1)}, u32[]{:S(2)}, u32[]{:S(2)}) collective-permute-start(f32[296,128]{1,0:T(8,128)S(1)} %add.18), channel_id=1, source_target_pairs={{0,12},{4,8},{8,4},{12,0},{1,13},{5,9},{9,5},{13,1},{2,14},{6,10},... | collective-permute-start | bytes 454664 | tf_op jit(solution)/shard_map/ppermute | solution.py:292
  59.1 5.4 %copy-start.1 = (f32[384,128]{1,0:T(8,128)S(1)}, f32[384,128]{1,0:T(8,128)}, u32[]{:S(2)}) copy-start(f32[384,128]{1,0:T(8,128)} %get-tuple-element.26) | copy-start | bytes 589828
  59.1 5.3 %collective-permute-start.11 = (f32[296,128]{1,0:T(8,128)S(1)}, f32[296,128]{1,0:T(8,128)S(1)}, u32[]{:S(2)}, u32[]{:S(2)}) collective-permute-start(f32[296,128]{1,0:T(8,128)S(1)} %add.19), channel_id=1, source_target_pairs={{0,2},{1,3},{2,0},{3,1},{4,6},{5,7},{6,4},{7,5},{8,10},{9,11},{10,... | collective-permute-start | bytes 454664 | tf_op jit(solution)/shard_map/ppermute | solution.py:292
  64.4 7.5 %collective-permute-start.12 = (f32[592,128]{1,0:T(8,128)S(1)}, f32[592,128]{1,0:T(8,128)S(1)}, u32[]{:S(2)}, u32[]{:S(2)}) collective-permute-start(f32[592,128]{1,0:T(8,128)S(1)} %maximum_select_fusion.1), channel_id=1, source_target_pairs={{0,1},{1,0},{2,3},{3,2},{4,5},{5,4},{6,7},{7,6},{8,9},{9,8},{10,11... | collective-permute-start | bytes 909320 | tf_op jit(solution)/shard_map/ppermute | solution.py:292
  64.5 5.3 %copy-start.8 = (s32[1,1,1,6,64]{4,2,3,1,0:T(1,128)S(1)}, s32[1,1,1,6,64]{4,2,3,1,0:T(1,128)}, u32[]{:S(2)}) copy-start(s32[1,1,1,6,64]{4,2,3,1,0:T(1,128)} %param.22) | copy-start | bytes 4612
  64.6 5.9 %collective-permute-start.5 = (f32[64,128]{1,0:T(8,128)S(1)}, f32[64,128]{1,0:T(8,128)S(1)}, u32[]{:S(2)}, u32[]{:S(2)}) collective-permute-start(f32[64,128]{1,0:T(8,128)S(1)} %get-tuple-element.39), channel_id=1, source_target_pairs={{0,3},{1,0},{2,1},{3,2},{4,7},{5,4},{6,5},{7,6},{8,11},{9,8},{10,9... | collective-permute-start | bytes 98312 | tf_op jit(solution)/shard_map/ppermute | solution.py:16
  66.2 7.1 %collective-permute-start.4 = (f32[64,128]{1,0:T(8,128)S(1)}, f32[64,128]{1,0:T(8,128)S(1)}, u32[]{:S(2)}, u32[]{:S(2)}) collective-permute-start(f32[64,128]{1,0:T(8,128)S(1)} %get-tuple-element.40), channel_id=1, source_target_pairs={{0,1},{1,2},{2,3},{3,0},{4,5},{5,6},{6,7},{7,4},{8,9},{9,10},{10,1... | collective-permute-start | bytes 98312 | tf_op jit(solution)/shard_map/ppermute | solution.py:16
  66.2 7.1 %collective-permute-start.3 = (f32[64,128]{1,0:T(8,128)S(1)}, f32[64,128]{1,0:T(8,128)S(1)}, u32[]{:S(2)}, u32[]{:S(2)}) collective-permute-start(f32[64,128]{1,0:T(8,128)S(1)} %get-tuple-element.41), channel_id=1, source_target_pairs={{0,12},{4,0},{8,4},{12,8},{1,13},{5,1},{9,5},{13,9},{2,14},{6,2},{... | collective-permute-start | bytes 98312 | tf_op jit(solution)/shard_map/ppermute | solution.py:16
  69.8 5.7 %collective-permute-start.2 = (f32[64,128]{1,0:T(8,128)S(1)}, f32[64,128]{1,0:T(8,128)S(1)}, u32[]{:S(2)}, u32[]{:S(2)}) collective-permute-start(f32[64,128]{1,0:T(8,128)S(1)} %get-tuple-element.42), channel_id=1, source_target_pairs={{0,4},{4,8},{8,12},{12,0},{1,5},{5,9},{9,13},{13,1},{2,6},{6,10},{... | collective-permute-start | bytes 98312 | tf_op jit(solution)/shard_map/ppermute | solution.py:16
  70.4 2.9 %copy-start.2 = (f32[64,128]{1,0:T(8,128)}, f32[64,128]{1,0:T(8,128)S(1)}, u32[]{:S(2)}) copy-start(f32[64,128]{1,0:T(8,128)S(1)} %collective-permute-done.5.r5_ref) | copy-start | bytes 98308
  70.4 5.1 %collective-permute-start.1 = (f32[64,128]{1,0:T(8,128)S(1)}, f32[64,128]{1,0:T(8,128)S(1)}, u32[]{:S(2)}, u32[]{:S(2)}) collective-permute-start(f32[64,128]{1,0:T(8,128)S(1)} %get-tuple-element.43), channel_id=1, source_target_pairs={{0,16},{16,0},{1,17},{17,1},{2,18},{18,2},{3,19},{19,3},{4,20},{20... | collective-permute-start | bytes 98312 | tf_op jit(solution)/shard_map/ppermute | solution.py:16
  72.0 3.9 %collective-permute-start = (f32[64,128]{1,0:T(8,128)S(1)}, f32[64,128]{1,0:T(8,128)S(1)}, u32[]{:S(2)}, u32[]{:S(2)}) collective-permute-start(f32[64,128]{1,0:T(8,128)S(1)} %get-tuple-element.44), channel_id=1, source_target_pairs={{0,16},{16,0},{1,17},{17,1},{2,18},{18,2},{3,19},{19,3},{4,20},{20... | collective-permute-start | bytes 98312 | tf_op jit(solution)/shard_map/ppermute | solution.py:16
  73.4 2.5 %copy-start.3 = (f32[64,128]{1,0:T(8,128)}, f32[64,128]{1,0:T(8,128)S(1)}, u32[]{:S(2)}) copy-start(f32[64,128]{1,0:T(8,128)S(1)} %collective-permute-done.4.r4_ref) | copy-start | bytes 98308
  73.4 2.5 %copy-start.4 = (f32[64,128]{1,0:T(8,128)}, f32[64,128]{1,0:T(8,128)S(1)}, u32[]{:S(2)}) copy-start(f32[64,128]{1,0:T(8,128)S(1)} %collective-permute-done.3.r3_ref) | copy-start | bytes 98308
  75.5 0.6 copy-start.5
  75.5 0.6 copy-start.6
  75.9 0.6 copy-start.7
